TPU v7x, 32 devices: a whole 2x2x4 slice. The times are simulated.
32 devices in a mesh: tm: 4 (over z), env: 8 (over y, x, core).
Axes of the slice: x: 2, y: 2, z: 4, core: 2. Of those that a mesh axis runs over, the one named last changes fastest.
Arguments:
- rewards: float32 [1024, 1024], P('tm', 'env'), may hold values from -6 to 6
- dones: int32 [1024, 1024], P('tm', 'env'), may hold values 0 or 1
- horizon: float32 [1024], P('env'), may hold values from 20 to 2048
- bootstrap: float32 [1024], P('env'), may hold values from -96 to 96
- prior_mean: float32 [1], replicated, may hold values from -240 to 240
- prior_var: float32 [1], replicated, may hold values from 100 to 3000
Outputs:
- scaled_rewards: float32 [1024, 1024], P('tm', 'env')
- scaled_returns: float32 [1024, 1024], P('tm', 'env')
- running_stats: float32 [2], replicated
All inputs are finite; a program needn't handle non-finite values. No bound on the sum of `dones` on one device may be relied on, other than what follows from the above.
Results may differ from a plain program's by a relative error of at most 0.0003.
Values sent between devices are 32-bit elements; how exact they have to be, the bound alone decides.
A program may use at most 64 MiB of HBM per device.

v0:
```python
import jax
import jax.numpy as jnp
from jax import lax
from jax.sharding import PartitionSpec as P


def passed_along(value, axis, steps):
    count = lax.axis_size(axis)
    first, last = (max(0, -steps), min(count, count - steps))
    return lax.ppermute(value, axis, [(source, source + steps) for source in range(first, last)])


def compose(earlier, later):
    return (later[0] + later[1] * earlier[0], later[1] * earlier[1])


def local_returns(rewards, factor):
    summed, product = lax.associative_scan(compose, (rewards[::-1], factor[::-1]), axis=0)
    return (summed[::-1], product[::-1])


def combine_moments(former, latter):
    merged = former[0] + latter[0]
    delta = latter[1] - former[1]
    new_mean = former[1] + delta * latter[0] / merged
    new_spread = former[2] + latter[2] + delta * delta * former[0] * latter[0] / merged
    return (merged, new_mean, new_spread)


def batch_moments(returns, center, total_entries):
    centered = returns - center
    first_sum, second_sum = lax.psum(
        (jnp.sum(centered), jnp.sum(centered * centered)), ("tm", "env")
    )
    entries = jnp.float32(total_entries)
    average = center + first_sum / entries
    spread = second_sum - first_sum * first_sum / entries
    return (entries, average, spread)


def finish(batch, prior_mean, prior_var, total_entries):
    prior_count = jnp.float32(total_entries)
    merged, new_mean, new_spread = combine_moments(
        (prior_count, prior_mean[0], prior_var[0] * prior_count), batch
    )
    variance = new_spread / merged
    inverse = 1.0 / jnp.sqrt(variance + 1e-08)
    return (new_mean, variance, inverse)


def local(rewards, dones, horizon, bootstrap, prior_mean, prior_var):
    discount = 1.0 - 1.0 / horizon
    factor = discount[None, :] * (1.0 - dones.astype(jnp.float32))
    time_blocks = lax.axis_size("tm")
    total_entries = rewards.shape[0] * time_blocks * rewards.shape[1] * lax.axis_size("env")
    position = lax.axis_index("tm")
    summed, product = local_returns(rewards, factor)
    first_sum = summed[0]
    first_product = product[0]
    is_last = position == time_blocks - 1

    def chain_step(index, state):
        passed, received = state
        incoming = passed_along(passed, "tm", -1)
        received = jnp.where(is_last, bootstrap, incoming)
        return (first_sum + first_product * received, received)

    zeros_env = jnp.zeros_like(bootstrap)
    passed, arrived = lax.fori_loop(0, time_blocks, chain_step, (zeros_env, zeros_env))
    returns = summed + product * arrived[None, :]
    batch = batch_moments(returns, prior_mean[0], total_entries)
    new_mean, variance, inverse = finish(batch, prior_mean, prior_var, total_entries)
    return (rewards * inverse, returns * inverse, jnp.stack([new_mean, variance]))


def solution(mesh):
    return jax.shard_map(
        local,
        mesh=mesh,
        in_specs=(P("tm", "env"), P("tm", "env"), P("env"), P("env"), P(), P()),
        out_specs=(P("tm", "env"), P("tm", "env"), P()),
        check_vma=False,
    )
```

profile of v0, /device:TPU:0, one launch (start us, length us, event | category | flops | bytes accessed | tf_op | source)
XLA Modules:
  0.0 80.2 jit_solution(9871802101668938880)
XLA Ops:
  1.9 0.0 copy-start.4
  1.9 0.6 copy-done.4
  2.6 0.7 slice.258
  3.3 0.0 copy-start
  3.3 1.0 %slice.263 = f32[128,128]{1,0:T(8,128)S(1)} slice(f32[256,128]{1,0:T(8,128)} %param.8), slice={[0:255:2], [0:128:1]} | slice | bytes 131072 | tf_op jit(solution)/shard_map/slice | solution.py:18
  4.3 0.0 copy-done
  4.3 0.0 copy-start.1
  4.4 0.9 %copy-done.1 = s32[256,128]{1,0:T(8,128)S(1)} copy-done((s32[256,128]{1,0:T(8,128)S(1)}, s32[256,128]{1,0:T(8,128)}, u32[]{:S(2)}) %copy-start.1) | copy-done | bytes 131096
  7.2 0.1 rev.9
  7.3 0.0 copy-start.2
  7.3 0.1 rev.8
  7.4 0.6 copy-done.2
  8.0 25.2 %while.13 = (s32[]{:T(128)}, f32[128]{0:T(128)S(1)}, f32[128]{0:T(128)}, pred[]{:T(512)}, f32[128]{0:T(128)S(1)}, /*index=5*/f32[128]{0:T(128)S(1)}, f32[128]{0:T(128)S(1)}, s32[]{:T(128)}, s32[]{:T(128)}) while((s32[]{:T(128)}, f32[128]{0:T(128)S(1)}, f32[128]{0:T(128)}, pred[]{:T(512)}, f32[128]{0:T(128)S(1)}, ...), condition=%wide.region_1.2_spmd.clone, body=%wide.region_0.1_spmd.clone.sunk | while | flops 515 | bytes 6288 | solution.py:69
  8.0 1.3 %collective-permute-start = (f32[128]{0:T(128)S(1)}, f32[128]{0:T(128)S(1)}, u32[]{:S(2)}, u32[]{:S(2)}) collective-permute-start(f32[128]{0:T(128)S(1)} %broadcast_select_fusion.4), channel_id=1, source_target_pairs={{8,0},{16,8},{24,16},{9,1},{17,9},{25,17},{10,2},{18,10},{26,18},{... | collective-permute-start | bytes 1544 | tf_op jit(solution)/shard_map/while/body/eval_jaxpr/ppermute | solution.py:10
  9.3 5.2 %collective-permute-done = f32[128]{0:T(128)S(1)} collective-permute-done((f32[128]{0:T(128)S(1)}, f32[128]{0:T(128)S(1)}, u32[]{:S(2)}, u32[]{:S(2)}) %collective-permute-start) | collective-permute-done | bytes 544 | tf_op jit(solution)/shard_map/while/body/eval_jaxpr/ppermute | solution.py:10
  14.5 0.6 multiply_add_fusion.15
  15.1 1.3 %collective-permute-start = (f32[128]{0:T(128)S(1)}, f32[128]{0:T(128)S(1)}, u32[]{:S(2)}, u32[]{:S(2)}) collective-permute-start(f32[128]{0:T(128)S(1)} %broadcast_select_fusion.4), channel_id=1, source_target_pairs={{8,0},{16,8},{24,16},{9,1},{17,9},{25,17},{10,2},{18,10},{26,18},{... | collective-permute-start | bytes 1544 | tf_op jit(solution)/shard_map/while/body/eval_jaxpr/ppermute | solution.py:10
  16.4 4.2 %collective-permute-done = f32[128]{0:T(128)S(1)} collective-permute-done((f32[128]{0:T(128)S(1)}, f32[128]{0:T(128)S(1)}, u32[]{:S(2)}, u32[]{:S(2)}) %collective-permute-start) | collective-permute-done | bytes 544 | tf_op jit(solution)/shard_map/while/body/eval_jaxpr/ppermute | solution.py:10
  20.5 0.6 multiply_add_fusion.15
  21.1 1.3 %collective-permute-start = (f32[128]{0:T(128)S(1)}, f32[128]{0:T(128)S(1)}, u32[]{:S(2)}, u32[]{:S(2)}) collective-permute-start(f32[128]{0:T(128)S(1)} %broadcast_select_fusion.4), channel_id=1, source_target_pairs={{8,0},{16,8},{24,16},{9,1},{17,9},{25,17},{10,2},{18,10},{26,18},{... | collective-permute-start | bytes 1544 | tf_op jit(solution)/shard_map/while/body/eval_jaxpr/ppermute | solution.py:10
  22.4 4.2 %collective-permute-done = f32[128]{0:T(128)S(1)} collective-permute-done((f32[128]{0:T(128)S(1)}, f32[128]{0:T(128)S(1)}, u32[]{:S(2)}, u32[]{:S(2)}) %collective-permute-start) | collective-permute-done | bytes 544 | tf_op jit(solution)/shard_map/while/body/eval_jaxpr/ppermute | solution.py:10
  26.6 0.6 multiply_add_fusion.15
  27.2 1.3 %collective-permute-start = (f32[128]{0:T(128)S(1)}, f32[128]{0:T(128)S(1)}, u32[]{:S(2)}, u32[]{:S(2)}) collective-permute-start(f32[128]{0:T(128)S(1)} %broadcast_select_fusion.4), channel_id=1, source_target_pairs={{8,0},{16,8},{24,16},{9,1},{17,9},{25,17},{10,2},{18,10},{26,18},{... | collective-permute-start | bytes 1544 | tf_op jit(solution)/shard_map/while/body/eval_jaxpr/ppermute | solution.py:10
  28.5 4.2 %collective-permute-done = f32[128]{0:T(128)S(1)} collective-permute-done((f32[128]{0:T(128)S(1)}, f32[128]{0:T(128)S(1)}, u32[]{:S(2)}, u32[]{:S(2)}) %collective-permute-start) | collective-permute-done | bytes 544 | tf_op jit(solution)/shard_map/while/body/eval_jaxpr/ppermute | solution.py:10
  32.6 0.6 multiply_add_fusion.15
  33.2 0.0 copy-start.3
  33.2 0.7 copy-done.3
  33.9 0.7 subtract_reduce_fusion
  34.6 41.1 %all-reduce.32 = (f32[]{:T(128)}, f32[]{:T(128)}) all-reduce(f32[]{:T(128)} %get-tuple-element.64, f32[]{:T(128)} %get-tuple-element.63), channel_id=1, replica_groups=mesh['tm'=4,'env'=8] {'tm','env'}, use_global_device_ids=true, to_apply=%region_3.4 | all-reduce | flops 2 | bytes 16 | tf_op jit(solution)/shard_map/psum | solution.py:32
  78.3 0.7 broadcast_multiply_fusion
  78.9 0.6 pad_maximum_fusion.14
  79.5 0.7 broadcast_multiply_fusion.1
  (138 shorter events, 1.4 us)
Async XLA Ops:
  1.9 0.7 copy-start.4
  3.3 1.0 %copy-start = (f32[256,128]{1,0:T(8,128)S(1)}, f32[256,128]{1,0:T(8,128)}, u32[]{:S(2)}) copy-start(f32[256,128]{1,0:T(8,128)} %param.8) | copy-start | bytes 393220
  4.3 0.9 %copy-start.1 = (s32[256,128]{1,0:T(8,128)S(1)}, s32[256,128]{1,0:T(8,128)}, u32[]{:S(2)}) copy-start(s32[256,128]{1,0:T(8,128)} %param.9) | copy-start | bytes 393220
  7.3 0.7 copy-start.2
  8.0 6.5 %collective-permute-start = (f32[128]{0:T(128)S(1)}, f32[128]{0:T(128)S(1)}, u32[]{:S(2)}, u32[]{:S(2)}) collective-permute-start(f32[128]{0:T(128)S(1)} %broadcast_select_fusion.4), channel_id=1, source_target_pairs={{8,0},{16,8},{24,16},{9,1},{17,9},{25,17},{10,2},{18,10},{26,18},{... | collective-permute-start | bytes 1544 | tf_op jit(solution)/shard_map/while/body/eval_jaxpr/ppermute | solution.py:10
  15.1 5.5 %collective-permute-start = (f32[128]{0:T(128)S(1)}, f32[128]{0:T(128)S(1)}, u32[]{:S(2)}, u32[]{:S(2)}) collective-permute-start(f32[128]{0:T(128)S(1)} %broadcast_select_fusion.4), channel_id=1, source_target_pairs={{8,0},{16,8},{24,16},{9,1},{17,9},{25,17},{10,2},{18,10},{26,18},{... | collective-permute-start | bytes 1544 | tf_op jit(solution)/shard_map/while/body/eval_jaxpr/ppermute | solution.py:10
  21.1 5.5 %collective-permute-start = (f32[128]{0:T(128)S(1)}, f32[128]{0:T(128)S(1)}, u32[]{:S(2)}, u32[]{:S(2)}) collective-permute-start(f32[128]{0:T(128)S(1)} %broadcast_select_fusion.4), channel_id=1, source_target_pairs={{8,0},{16,8},{24,16},{9,1},{17,9},{25,17},{10,2},{18,10},{26,18},{... | collective-permute-start | bytes 1544 | tf_op jit(solution)/shard_map/while/body/eval_jaxpr/ppermute | solution.py:10
  27.2 5.5 %collective-permute-start = (f32[128]{0:T(128)S(1)}, f32[128]{0:T(128)S(1)}, u32[]{:S(2)}, u32[]{:S(2)}) collective-permute-start(f32[128]{0:T(128)S(1)} %broadcast_select_fusion.4), channel_id=1, source_target_pairs={{8,0},{16,8},{24,16},{9,1},{17,9},{25,17},{10,2},{18,10},{26,18},{... | collective-permute-start | bytes 1544 | tf_op jit(solution)/shard_map/while/body/eval_jaxpr/ppermute | solution.py:10
  33.2 0.7 copy-start.3
where the time goes:
time: 80.7 us; the launch traced here: 80.2 us
  blocking collectives  41.1 us (51%)
  waiting for transfers between devices  17.7 us (22%)
  local copies, waits for them, and re-layouts  5.57 us (7%)
  other arithmetic  5.46 us (7%)
  between operations  5.2 us (6%)
  starting transfers between devices  5.12 us (6%)
    psum x1, blocking collectives, batch_moments(): lax.psum((jnp.sum(centered), jnp.sum(centered * centered)), ('tm', 'env'))  41.1 us
    ppermute x4, waiting for transfers between devices, passed_along(): lax.ppermute(value, axis, [(source, source + steps) for source in range(f...  17.7 us
    ppermute x4, starting transfers between devices, passed_along(): lax.ppermute(value, axis, [(source, source + steps) for source in range(f...  5.12 us
    unnamed x10, local copies, waits for them, and re-layouts  2.75 us
    slice x58, local copies, waits for them, and re-layouts, local_returns(): lax.associative_scan(compose, (rewards[::-1], factor[::-1]), axis=0)  2.41 us
    add x4, other arithmetic, chain_step(): return (first_sum + first_product * received, received)  2.36 us
  transfers between devices with their start and end apart: 4, of which 4 were waited for; matrix products, arithmetic and copies ran while one was open for 0% of the time, Pallas kernels for 0%

commit v1 on v0

v1 whole, which is shorter than its diff:
```python
import functools

import jax
import jax.numpy as jnp
from jax import lax
from jax.experimental import pallas as pl
from jax.experimental.pallas import tpu as pltpu
from jax.sharding import PartitionSpec as P

SUB = 8
ROWS = 8


def compose_rows(summed, product, row):
    step = 1
    while step < SUB:
        inside = row < SUB - step
        later_sum = jnp.where(inside, pltpu.roll(summed, SUB - step, 0), 0.0)
        later_product = jnp.where(inside, pltpu.roll(product, SUB - step, 0), 1.0)
        summed = summed + product * later_sum
        product = product * later_product
        step *= 2
    return summed, product


def kernel(T, E, rewards_hbm, dones_hbm, horizon_ref, bootstrap_ref, mean_ref, var_ref,
           returns_ref, inverse_ref, stats_ref,
           rewards, dones, s_buf, p_buf, tbuf, ebuf, load_sem, tsend, trecv, esend, erecv):
    t = lax.axis_index("tm")
    e = lax.axis_index("env")
    barrier = pltpu.get_barrier_semaphore()
    for d in range(1, T):
        pl.semaphore_signal(barrier, inc=1, device_id={"tm": lax.rem(t + d, T)},
                            device_id_type=pl.DeviceIdType.MESH)
    for d in range(1, E):
        pl.semaphore_signal(barrier, inc=1, device_id={"env": lax.rem(e + d, E)},
                            device_id_type=pl.DeviceIdType.MESH)
    loads = [pltpu.make_async_copy(rewards_hbm, rewards, load_sem.at[0]),
             pltpu.make_async_copy(dones_hbm, dones, load_sem.at[1])]
    for load in loads:
        load.start()
    rows, lanes = rewards.shape
    chunk = rows // SUB
    shape = (SUB, lanes)
    row = lax.broadcasted_iota(jnp.int32, shape, 0)
    discount = jnp.broadcast_to(1.0 - 1.0 / horizon_ref[...], shape)
    center = jnp.broadcast_to(mean_ref[...], shape)
    for load in loads:
        load.wait()
    s = jnp.zeros(shape, jnp.float32)
    p = jnp.ones(shape, jnp.float32)
    zero = jnp.zeros(shape, jnp.float32)
    s1, p1, s2, sp, p2 = zero, zero, zero, zero, zero
    for k in reversed(range(chunk)):
        r = rewards[pl.ds(k, SUB, stride=chunk), :]
        f = jnp.where(dones[pl.ds(k, SUB, stride=chunk), :] == 0, discount, 0.0)
        s = r + f * s
        p = f * p
        s_buf[k] = s
        p_buf[k] = p
        c = s - center
        s1 = s1 + c
        p1 = p1 + p
        s2 = s2 + c * c
        sp = sp + c * p
        p2 = p2 + p * p
    full_s, full_p = compose_rows(s, p, row)
    last = row == SUB - 1
    a = jnp.where(last, 0.0, pltpu.roll(full_s, SUB - 1, 0))
    b = jnp.where(last, 1.0, pltpu.roll(full_p, SUB - 1, 0))
    down = lambda value: jnp.sum(value, axis=0, keepdims=True)
    tbuf[t, 0:1] = full_s[0:1]
    tbuf[t, 1:2] = full_p[0:1]
    tbuf[t, 2:3] = down(s1 + p1 * a)
    tbuf[t, 3:4] = down(p1 * b)
    tbuf[t, 4:5] = down(s2 + a * (2.0 * sp + a * p2))
    tbuf[t, 5:6] = down(2.0 * b * (sp + a * p2))
    tbuf[t, 6:7] = down(b * b * p2)
    tbuf[t, 7:8] = jnp.zeros((1, lanes), jnp.float32)
    pl.semaphore_wait(barrier, T + E - 2)
    copies = []
    for d in range(1, T):
        copies.append(pltpu.make_async_remote_copy(
            tbuf.at[t], tbuf.at[t], tsend.at[d - 1], trecv.at[d - 1],
            device_id={"tm": lax.rem(t + d, T)}, device_id_type=pl.DeviceIdType.MESH))
    for copy in copies:
        copy.start()
    for copy in copies:
        copy.wait()
    x = bootstrap_ref[...]
    mine = x
    first = jnp.zeros((1, lanes), jnp.float32)
    second = jnp.zeros((1, lanes), jnp.float32)
    for j in reversed(range(T)):
        mine = jnp.where(t == j, x, mine)
        first = first + tbuf[j, 2:3] + tbuf[j, 3:4] * x
        second = second + tbuf[j, 4:5] + x * (tbuf[j, 5:6] + x * tbuf[j, 6:7])
        x = tbuf[j, 0:1] + tbuf[j, 1:2] * x
    ebuf[e, 0:1] = first
    ebuf[e, 1:2] = second
    copies = []
    for d in range(1, E):
        copies.append(pltpu.make_async_remote_copy(
            ebuf.at[e], ebuf.at[e], esend.at[d - 1], erecv.at[d - 1],
            device_id={"env": lax.rem(e + d, E)}, device_id_type=pl.DeviceIdType.MESH))
    for copy in copies:
        copy.start()
    y = a + b * mine
    for k in range(chunk):
        returns_ref[pl.ds(k, SUB, stride=chunk), :] = s_buf[k] + p_buf[k] * y
    for copy in copies:
        copy.wait()
    total = ebuf[0]
    for j in range(1, E):
        total = total + ebuf[j]
    sums = jnp.sum(total, axis=1, keepdims=True)
    entries = jnp.float32(rows * T * lanes * E)
    first = sums[0:1]
    second = sums[1:2]
    mean0 = mean_ref[...]
    average = mean0 + first / entries
    spread = second - first * first / entries
    prior_count = entries
    merged = prior_count + entries
    delta = average - mean0
    new_mean = mean0 + delta * entries / merged
    new_spread = var_ref[...] * prior_count + spread + delta * delta * prior_count * entries / merged
    variance = new_spread / merged
    inverse_ref[...] = jnp.broadcast_to(1.0 / jnp.sqrt(variance + 1e-08), inverse_ref.shape)
    lane = lax.broadcasted_iota(jnp.int32, (1, lanes), 1)
    stats_ref[...] = jnp.where(lane == 0, new_mean, variance)


def local(T, E, rewards, dones, horizon, bootstrap, prior_mean, prior_var):
    rows, lanes = rewards.shape
    vmem = pl.BlockSpec(memory_space=pltpu.VMEM)
    hbm = pl.BlockSpec(memory_space=pl.ANY)
    returns, inverse, stats = pl.pallas_call(
        functools.partial(kernel, T, E),
        out_shape=(jax.ShapeDtypeStruct((rows, lanes), jnp.float32),
                   jax.ShapeDtypeStruct((1, lanes), jnp.float32),
                   jax.ShapeDtypeStruct((1, lanes), jnp.float32)),
        in_specs=[hbm, hbm, vmem, vmem, vmem, vmem],
        out_specs=(vmem, vmem, vmem),
        scratch_shapes=[
            pltpu.VMEM((rows, lanes), jnp.float32),
            pltpu.VMEM((rows, lanes), jnp.int32),
            pltpu.VMEM((rows // SUB, SUB, lanes), jnp.float32),
            pltpu.VMEM((rows // SUB, SUB, lanes), jnp.float32),
            pltpu.VMEM((T, ROWS, lanes), jnp.float32),
            pltpu.VMEM((E, 2, lanes), jnp.float32),
            pltpu.SemaphoreType.DMA((2,)),
            pltpu.SemaphoreType.DMA((T - 1,)),
            pltpu.SemaphoreType.DMA((T - 1,)),
            pltpu.SemaphoreType.DMA((E - 1,)),
            pltpu.SemaphoreType.DMA((E - 1,)),
        ],
        compiler_params=pltpu.CompilerParams(collective_id=0, has_side_effects=True),
    )(rewards, dones, horizon.reshape(1, lanes), bootstrap.reshape(1, lanes),
      prior_mean.reshape(1, 1), prior_var.reshape(1, 1))
    return (rewards * inverse, returns * inverse, stats[0, :2])


def solution(mesh):
    T, E = mesh.shape["tm"], mesh.shape["env"]
    return jax.shard_map(
        functools.partial(local, T, E),
        mesh=mesh,
        in_specs=(P("tm", "env"), P("tm", "env"), P("env"), P("env"), P(), P()),
        out_specs=(P("tm", "env"), P("tm", "env"), P()),
        check_vma=False,
    )
```

time: 80.7 us -> 18.5 us (0.23)
  blocking collectives: 41.1 us -> 0 us
  waiting for transfers between devices: 17.7 us -> 0 us
  Pallas kernels: 0 us -> 13.5 us
  starting transfers between devices: 5.12 us -> 0 us
  local copies, waits for them, and re-layouts: 5.57 us -> 1.22 us
  other arithmetic: 5.46 us -> 1.62 us
  between operations: 5.2 us -> 1.95 us
    psum x1 -> x0, blocking collectives: 41.1 us -> none  [batch_moments(): lax.psum((jnp.sum(centered), jnp.sum(centered * centered)), ('tm', 'env'))]
    ppermute x4 -> x0, waiting for transfers between devices: 17.7 us -> none  [passed_along(): lax.ppermute(value, axis, [(source, source + steps) for source in range(f...]
    pallas_call x0 -> x1, Pallas kernels: none -> 13.5 us  [local(): pl.pallas_call(functools.partial(kernel, T, E), out_shape=(jax.ShapeDtype...]
    ppermute x4 -> x0, starting transfers between devices: 5.12 us -> none  [passed_along(): lax.ppermute(value, axis, [(source, source + steps) for source in range(f...]
    add x19 -> x0, other arithmetic: 2.49 us -> none  [the longest x4 2.36 us: chain_step(): return (first_sum + first_product * received, received)]
    slice x58 -> x0, local copies, waits for them, and re-layouts: 2.41 us -> none  [local_returns(): lax.associative_scan(compose, (rewards[::-1], factor[::-1]), axis=0)]
    unnamed x10 -> x6, local copies, waits for them, and re-layouts: 2.75 us -> 0.71 us
    mul x17 -> x1, other arithmetic: 1.5 us -> 1.62 us  [local(): return (rewards * inverse, returns * inverse, stats[0, :2])]
  transfers between devices with their start and end apart: 4 -> 0, of which waited for: 4 -> 0; matrix products, arithmetic and copies ran while one was open for 0% -> 0% of each run, Pallas kernels for 0% -> 0%
where the time goes in v1:
time: 18.5 us; the launch traced here: 18.3 us
  Pallas kernels  13.5 us (73%)
  between operations  1.95 us (11%)
  other arithmetic  1.62 us (9%)
  local copies, waits for them, and re-layouts  1.22 us (7%)
    pallas_call x1, Pallas kernels, local(): pl.pallas_call(functools.partial(kernel, T, E), out_shape=(jax.ShapeDtype...  13.5 us
    mul x1, other arithmetic, local(): return (rewards * inverse, returns * inverse, stats[0, :2])  1.62 us
    unnamed x6, local copies, waits for them, and re-layouts  0.71 us
    squeeze x1, local copies, waits for them, and re-layouts, local(): return (rewards * inverse, returns * inverse, stats[0, :2])  0.51 us

profile of v1, /device:TPU:0, one launch (start us, length us, event | category | flops | bytes accessed | tf_op | source)
XLA Modules:
  0.0 18.3 jit_solution(17434650632267828363)
XLA Ops:
  1.9 0.0 copy-start
  1.9 13.5 %shard_map.85 = (f32[256,128]{1,0:T(8,128)}, f32[1,128]{1,0:T(1,128)}, f32[1,128]{1,0:T(1,128)}) custom-call(f32[256,128]{1,0:T(8,128)} %rewards_hbm.1, s32[256,128]{1,0:T(8,128)} %dones_hbm.1, f32[1,128]{1,0:T(1,128)} %bitcast.9, f32[1,128]{1,0:T(1,128)} %bitcast.10, f32[1,1]{1,0:T(1,128)} %bitcast.7.mean_ref, f32[1,1]{1,0:T(1,128)} %bitcast.8.var_ref), custom_call_target="tpu_custom_call" | custom-call | tf_op jit(solution)/shard_map/pallas_call | solution.py:138
  15.4 0.0 copy-start.2
  15.4 0.6 %copy-done.2 = f32[1,128]{1,0:T(1,128)S(1)} copy-done((f32[1,128]{1,0:T(1,128)S(1)}, f32[1,128]{1,0:T(1,128)}, u32[]{:S(2)}) %copy-start.2) | copy-done | bytes 536
  16.0 0.0 copy-start.1
  16.0 0.5 %slice_bitcast_fusion = f32[2]{0:T(128)} fusion(f32[1,128]{1,0:T(1,128)S(1)} %copy-done.2), kind=kLoop, calls=%fused_computation.2 | loop fusion | bytes 16 | tf_op jit(solution)/shard_map/squeeze | solution.py:161
  16.5 0.0 copy-done
  16.5 0.1 copy-done.1
  16.6 1.6 %broadcast_multiply_fusion = (f32[256,128]{1,0:T(8,128)}, f32[256,128]{1,0:T(8,128)}) fusion(f32[256,128]{1,0:T(8,128)} %get-tuple-element.7, f32[128]{0:T(128)S(1)} %bitcast.11, f32[256,128]{1,0:T(8,128)S(1)} %copy-done), kind=kLoop, calls=%fused_computation | loop fusion | flops 65536 | bytes 524800 | tf_op jit(solution)/shard_map/mul | solution.py:161
Async XLA Ops:
  1.9 14.6 %copy-start = (f32[256,128]{1,0:T(8,128)S(1)}, f32[256,128]{1,0:T(8,128)}, u32[]{:S(2)}) copy-start(f32[256,128]{1,0:T(8,128)} %rewards_hbm.1) | copy-start | bytes 393220
  15.4 0.6 %copy-start.2 = (f32[1,128]{1,0:T(1,128)S(1)}, f32[1,128]{1,0:T(1,128)}, u32[]{:S(2)}) copy-start(f32[1,128]{1,0:T(1,128)} %get-tuple-element.8) | copy-start | bytes 1540
  16.0 0.6 %copy-start.1 = (f32[1,128]{1,0:T(1,128)S(1)}, f32[1,128]{1,0:T(1,128)}, u32[]{:S(2)}) copy-start(f32[1,128]{1,0:T(1,128)} %get-tuple-element.6) | copy-start | bytes 1540

commit v2 on v1

--- a/solution.py
+++ b/solution.py
@@ -9,6 +9,7 @@
 
 SUB = 8
 ROWS = 8
+PARTS = 4
 
 
 def compose_rows(summed, product, row):
@@ -23,9 +24,10 @@
     return summed, product
 
 
-def kernel(T, E, rewards_hbm, dones_hbm, horizon_ref, bootstrap_ref, mean_ref, var_ref,
-           returns_ref, inverse_ref, stats_ref,
-           rewards, dones, s_buf, p_buf, tbuf, ebuf, load_sem, tsend, trecv, esend, erecv):
+def kernel(T, E, rewards_hbm, dones_hbm, horizon_hbm, bootstrap_hbm, mean_hbm, var_hbm,
+           rewards, returns_ref, ebuf, prior_ref,
+           dones, horizon_ref, bootstrap_ref, mean_ref, var_ref, s_buf, p_buf, tbuf,
+           load_sem, tsend, trecv, esend, erecv):
     t = lax.axis_index("tm")
     e = lax.axis_index("env")
     barrier = pltpu.get_barrier_semaphore()
@@ -35,18 +37,21 @@
     for d in range(1, E):
         pl.semaphore_signal(barrier, inc=1, device_id={"env": lax.rem(e + d, E)},
                             device_id_type=pl.DeviceIdType.MESH)
-    loads = [pltpu.make_async_copy(rewards_hbm, rewards, load_sem.at[0]),
-             pltpu.make_async_copy(dones_hbm, dones, load_sem.at[1])]
+    pairs = [(horizon_hbm, horizon_ref), (mean_hbm, mean_ref), (var_hbm, var_ref),
+             (bootstrap_hbm, bootstrap_ref), (rewards_hbm, rewards),
+             (dones_hbm, dones)]
+    loads = [pltpu.make_async_copy(source, target, load_sem.at[i])
+             for i, (source, target) in enumerate(pairs)]
     for load in loads:
         load.start()
     rows, lanes = rewards.shape
     chunk = rows // SUB
     shape = (SUB, lanes)
     row = lax.broadcasted_iota(jnp.int32, shape, 0)
-    discount = jnp.broadcast_to(1.0 - 1.0 / horizon_ref[...], shape)
-    center = jnp.broadcast_to(mean_ref[...], shape)
     for load in loads:
         load.wait()
+    discount = jnp.broadcast_to(1.0 - 1.0 / horizon_ref[...], shape)
+    center = jnp.full(shape, mean_ref[0], jnp.float32)
     s = jnp.zeros(shape, jnp.float32)
     p = jnp.ones(shape, jnp.float32)
     zero = jnp.zeros(shape, jnp.float32)
@@ -105,11 +110,18 @@
             device_id={"env": lax.rem(e + d, E)}, device_id_type=pl.DeviceIdType.MESH))
     for copy in copies:
         copy.start()
+    prior_ref[0:1] = center[0:1]
+    prior_ref[1:2] = jnp.full((1, lanes), var_ref[0], jnp.float32)
     y = a + b * mine
     for k in range(chunk):
         returns_ref[pl.ds(k, SUB, stride=chunk), :] = s_buf[k] + p_buf[k] * y
     for copy in copies:
         copy.wait()
+
+
+def finish(T, E, rewards, returns, ebuf, prior_ref, out_rewards, out_returns, stats_ref,
+           rewards_out, returns_out, sems):
+    rows, lanes = rewards.shape
     total = ebuf[0]
     for j in range(1, E):
         total = total + ebuf[j]
@@ -117,48 +129,77 @@
     entries = jnp.float32(rows * T * lanes * E)
     first = sums[0:1]
     second = sums[1:2]
-    mean0 = mean_ref[...]
+    mean0 = prior_ref[0:1, 0:1]
+    var0 = prior_ref[1:2, 0:1]
     average = mean0 + first / entries
     spread = second - first * first / entries
     prior_count = entries
     merged = prior_count + entries
     delta = average - mean0
     new_mean = mean0 + delta * entries / merged
-    new_spread = var_ref[...] * prior_count + spread + delta * delta * prior_count * entries / merged
+    new_spread = var0 * prior_count + spread + delta * delta * prior_count * entries / merged
     variance = new_spread / merged
-    inverse_ref[...] = jnp.broadcast_to(1.0 / jnp.sqrt(variance + 1e-08), inverse_ref.shape)
-    lane = lax.broadcasted_iota(jnp.int32, (1, lanes), 1)
-    stats_ref[...] = jnp.where(lane == 0, new_mean, variance)
+    inverse = jnp.broadcast_to(1.0 / jnp.sqrt(variance + 1e-08), (SUB, lanes))
+    copies = []
+    part = rows // PARTS
+    for i in range(PARTS):
+        for n, (source, staged, target) in enumerate(
+                ((rewards, rewards_out, out_rewards), (returns, returns_out, out_returns))):
+            for k in range(i * part, (i + 1) * part, SUB):
+                staged[k:k + SUB] = source[k:k + SUB] * inverse
+            where = pl.ds(i * part, part)
+            copy = pltpu.make_async_copy(staged.at[where], target.at[where], sems.at[n, i])
+            copy.start()
+            copies.append(copy)
+    stats_ref[0] = new_mean[0, 0]
+    stats_ref[1] = variance[0, 0]
+    for copy in copies:
+        copy.wait()
 
 
 def local(T, E, rewards, dones, horizon, bootstrap, prior_mean, prior_var):
     rows, lanes = rewards.shape
+    block = (rows, lanes)
     vmem = pl.BlockSpec(memory_space=pltpu.VMEM)
-    hbm = pl.BlockSpec(memory_space=pl.ANY)
-    returns, inverse, stats = pl.pallas_call(
+    smem = pl.BlockSpec(memory_space=pltpu.SMEM)
+    hbm = pl.BlockSpec(memory_space=pltpu.HBM)
+    kept, returns, sums, prior = pl.pallas_call(
         functools.partial(kernel, T, E),
-        out_shape=(jax.ShapeDtypeStruct((rows, lanes), jnp.float32),
-                   jax.ShapeDtypeStruct((1, lanes), jnp.float32),
-                   jax.ShapeDtypeStruct((1, lanes), jnp.float32)),
-        in_specs=[hbm, hbm, vmem, vmem, vmem, vmem],
-        out_specs=(vmem, vmem, vmem),
+        out_shape=(pltpu.VMEM(block, jnp.float32), pltpu.VMEM(block, jnp.float32),
+                   pltpu.VMEM((E, 2, lanes), jnp.float32), pltpu.VMEM((2, lanes), jnp.float32)),
+        in_specs=[hbm] * 6,
+        out_specs=(vmem, vmem, vmem, vmem),
         scratch_shapes=[
-            pltpu.VMEM((rows, lanes), jnp.float32),
-            pltpu.VMEM((rows, lanes), jnp.int32),
+            pltpu.VMEM(block, jnp.int32),
+            pltpu.VMEM((1, lanes), jnp.float32),
+            pltpu.VMEM((1, lanes), jnp.float32),
+            pltpu.SMEM((1,), jnp.float32),
+            pltpu.SMEM((1,), jnp.float32),
             pltpu.VMEM((rows // SUB, SUB, lanes), jnp.float32),
             pltpu.VMEM((rows // SUB, SUB, lanes), jnp.float32),
             pltpu.VMEM((T, ROWS, lanes), jnp.float32),
-            pltpu.VMEM((E, 2, lanes), jnp.float32),
-            pltpu.SemaphoreType.DMA((2,)),
+            pltpu.SemaphoreType.DMA((6,)),
             pltpu.SemaphoreType.DMA((T - 1,)),
             pltpu.SemaphoreType.DMA((T - 1,)),
             pltpu.SemaphoreType.DMA((E - 1,)),
             pltpu.SemaphoreType.DMA((E - 1,)),
         ],
         compiler_params=pltpu.CompilerParams(collective_id=0, has_side_effects=True),
-    )(rewards, dones, horizon.reshape(1, lanes), bootstrap.reshape(1, lanes),
-      prior_mean.reshape(1, 1), prior_var.reshape(1, 1))
-    return (rewards * inverse, returns * inverse, stats[0, :2])
+    )(rewards, dones, horizon.reshape(1, lanes), bootstrap.reshape(1, lanes), prior_mean, prior_var)
+    return pl.pallas_call(
+        functools.partial(finish, T, E),
+        out_shape=(jax.ShapeDtypeStruct(block, jnp.float32),
+                   jax.ShapeDtypeStruct(block, jnp.float32),
+                   jax.ShapeDtypeStruct((2,), jnp.float32)),
+        in_specs=[vmem] * 4,
+        out_specs=(hbm, hbm, smem),
+        scratch_shapes=[
+            pltpu.VMEM(block, jnp.float32),
+            pltpu.VMEM(block, jnp.float32),
+            pltpu.SemaphoreType.DMA((2, PARTS)),
+        ],
+        compiler_params=pltpu.CompilerParams(vmem_limit_bytes=4 * 2**20),
+    )(kept, returns, sums, prior)
 
 
 def solution(mesh):

time: 18.5 us -> 15.7 us (0.85)
  other arithmetic: 1.62 us -> 0 us
  local copies, waits for them, and re-layouts: 1.22 us -> 0 us
    mul x1 -> x0, other arithmetic: 1.62 us -> none  [local(): return (rewards * inverse, returns * inverse, stats[0, :2])]
    unnamed x6 -> x0, local copies, waits for them, and re-layouts: 0.71 us -> none
    squeeze x1 -> x0, local copies, waits for them, and re-layouts: 0.51 us -> none  [local(): return (rewards * inverse, returns * inverse, stats[0, :2])]
    pallas_call x1 -> x2, Pallas kernels: 13.5 us -> 13.6 us  [the longest x1 12.2 us: local(): pl.pallas_call(functools.partial(kernel, T, E), out_shape=(pltpu.VMEM(blo...]
where the time goes in v2:
time: 15.7 us; the launch traced here: 15.5 us
  Pallas kernels  13.6 us (87%)
  between operations  1.93 us (12%)
    pallas_call x1, Pallas kernels, local(): pl.pallas_call(functools.partial(kernel, T, E), out_shape=(pltpu.VMEM(blo...  12.2 us
    pallas_call x1, Pallas kernels, local(): pl.pallas_call(functools.partial(finish, T, E), out_shape=(jax.ShapeDtype...  1.42 us

profile of v2, /device:TPU:0, one launch (start us, length us, event | category | flops | bytes accessed | tf_op | source)
XLA Modules:
  0.0 15.5 jit_solution(9765009675830822889)
XLA Ops:
  1.9 12.2 %shard_map.85 = (f32[256,128]{1,0:T(8,128)S(1)}, f32[256,128]{1,0:T(8,128)S(1)}, f32[8,2,128]{2,1,0:T(2,128)S(1)}, f32[2,128]{1,0:T(2,128)S(1)}) custom-call(f32[256,128]{1,0:T(8,128)} %rewards_hbm.1, s32[256,128]{1,0:T(8,128)} %dones_hbm.1, f32[1,128]{1,0:T(1,128)} %bitcast.2, f32[1,128]{1,0:T(1,128)} %bitcast.3, f32[1]{0:T(128)S(6)} %copy.9.mean_hbm, ...), custom_call_target="tpu_custom_call" | custom-call | tf_op jit(solution)/shard_map/pallas_call | solution.py:166
  14.1 1.4 %shard_map.86 = (f32[256,128]{1,0:T(8,128)}, f32[256,128]{1,0:T(8,128)}, f32[2]{0:T(128)}) custom-call(f32[256,128]{1,0:T(8,128)S(1)} %get-tuple-element.7.rewards, f32[256,128]{1,0:T(8,128)S(1)} %get-tuple-element.8.returns, f32[8,2,128]{2,1,0:T(2,128)S(1)} %get-tuple-element.9.ebuf, f32[2,128]{1,0:T(2,128)S(1)} %get-tuple-element.10.prior_ref), custom_call_target="tpu_custom_call" | custom-call | tf_op jit(solution)/shard_map/pallas_call | solution.py:189

commit v3 on v2

--- a/solution.py
+++ b/solution.py
@@ -24,9 +24,9 @@
     return summed, product
 
 
-def kernel(T, E, rewards_hbm, dones_hbm, horizon_hbm, bootstrap_hbm, mean_hbm, var_hbm,
+def kernel(T, E, rewards_hbm, dones_hbm, horizon_hbm, bootstrap_hbm, prior_hbm,
            rewards, returns_ref, ebuf, prior_ref,
-           dones, horizon_ref, bootstrap_ref, mean_ref, var_ref, s_buf, p_buf, tbuf,
+           dones, horizon_ref, bootstrap_ref, s_buf, p_buf, tbuf,
            load_sem, tsend, trecv, esend, erecv):
     t = lax.axis_index("tm")
     e = lax.axis_index("env")
@@ -37,7 +37,7 @@
     for d in range(1, E):
         pl.semaphore_signal(barrier, inc=1, device_id={"env": lax.rem(e + d, E)},
                             device_id_type=pl.DeviceIdType.MESH)
-    pairs = [(horizon_hbm, horizon_ref), (mean_hbm, mean_ref), (var_hbm, var_ref),
+    pairs = [(horizon_hbm, horizon_ref), (prior_hbm, prior_ref),
              (bootstrap_hbm, bootstrap_ref), (rewards_hbm, rewards),
              (dones_hbm, dones)]
     loads = [pltpu.make_async_copy(source, target, load_sem.at[i])
@@ -51,7 +51,7 @@
     for load in loads:
         load.wait()
     discount = jnp.broadcast_to(1.0 - 1.0 / horizon_ref[...], shape)
-    center = jnp.full(shape, mean_ref[0], jnp.float32)
+    center = jnp.broadcast_to(prior_ref[0:1], shape)
     s = jnp.zeros(shape, jnp.float32)
     p = jnp.ones(shape, jnp.float32)
     zero = jnp.zeros(shape, jnp.float32)
@@ -110,8 +110,6 @@
             device_id={"env": lax.rem(e + d, E)}, device_id_type=pl.DeviceIdType.MESH))
     for copy in copies:
         copy.start()
-    prior_ref[0:1] = center[0:1]
-    prior_ref[1:2] = jnp.full((1, lanes), var_ref[0], jnp.float32)
     y = a + b * mine
     for k in range(chunk):
         returns_ref[pl.ds(k, SUB, stride=chunk), :] = s_buf[k] + p_buf[k] * y
@@ -163,29 +161,29 @@
     vmem = pl.BlockSpec(memory_space=pltpu.VMEM)
     smem = pl.BlockSpec(memory_space=pltpu.SMEM)
     hbm = pl.BlockSpec(memory_space=pltpu.HBM)
+    row = lax.broadcasted_iota(jnp.int32, (2, lanes), 0)
+    prior = jnp.where(row == 0, prior_mean, prior_var)
     kept, returns, sums, prior = pl.pallas_call(
         functools.partial(kernel, T, E),
         out_shape=(pltpu.VMEM(block, jnp.float32), pltpu.VMEM(block, jnp.float32),
                    pltpu.VMEM((E, 2, lanes), jnp.float32), pltpu.VMEM((2, lanes), jnp.float32)),
-        in_specs=[hbm] * 6,
+        in_specs=[hbm] * 5,
         out_specs=(vmem, vmem, vmem, vmem),
         scratch_shapes=[
             pltpu.VMEM(block, jnp.int32),
             pltpu.VMEM((1, lanes), jnp.float32),
             pltpu.VMEM((1, lanes), jnp.float32),
-            pltpu.SMEM((1,), jnp.float32),
-            pltpu.SMEM((1,), jnp.float32),
             pltpu.VMEM((rows // SUB, SUB, lanes), jnp.float32),
             pltpu.VMEM((rows // SUB, SUB, lanes), jnp.float32),
             pltpu.VMEM((T, ROWS, lanes), jnp.float32),
-            pltpu.SemaphoreType.DMA((6,)),
+            pltpu.SemaphoreType.DMA((5,)),
             pltpu.SemaphoreType.DMA((T - 1,)),
             pltpu.SemaphoreType.DMA((T - 1,)),
             pltpu.SemaphoreType.DMA((E - 1,)),
             pltpu.SemaphoreType.DMA((E - 1,)),
         ],
         compiler_params=pltpu.CompilerParams(collective_id=0, has_side_effects=True),
-    )(rewards, dones, horizon.reshape(1, lanes), bootstrap.reshape(1, lanes), prior_mean, prior_var)
+    )(rewards, dones, horizon.reshape(1, lanes), bootstrap.reshape(1, lanes), prior)
     return pl.pallas_call(
         functools.partial(finish, T, E),
         out_shape=(jax.ShapeDtypeStruct(block, jnp.float32),

time: 15.7 us -> 16.3 us (1.038)
  local copies, waits for them, and re-layouts: 0 us -> 0.63 us
    iota x0 -> x1, local copies, waits for them, and re-layouts: none -> 0.63 us  [local(): row = lax.broadcasted_iota(jnp.int32, (2, lanes), 0)]
where the time goes in v3:
time: 16.3 us; the launch traced here: 16.1 us
  Pallas kernels  13.5 us (83%)
  between operations  1.94 us (12%)
  local copies, waits for them, and re-layouts  0.63 us (4%)
    pallas_call x1, Pallas kernels, local(): pl.pallas_call(functools.partial(kernel, T, E), out_shape=(pltpu.VMEM(blo...  12.1 us
    pallas_call x1, Pallas kernels, local(): pl.pallas_call(functools.partial(finish, T, E), out_shape=(jax.ShapeDtype...  1.42 us
    iota x1, local copies, waits for them, and re-layouts, local(): row = lax.broadcasted_iota(jnp.int32, (2, lanes), 0)  0.63 us

profile of v3, /device:TPU:0, one launch (start us, length us, event | category | flops | bytes accessed | tf_op | source)
XLA Modules:
  0.0 16.1 jit_solution(8331373103049057518)
XLA Ops:
  1.9 0.6 %iota.7.prior_hbm = f32[2,128]{1,0:T(2,128)} broadcast(f32[2]{0:T(128)S(1)} %compare_select_fusion), dimensions={0} | broadcast | bytes 1032 | tf_op jit(solution)/shard_map/iota | solution.py:164
  2.6 12.1 %shard_map.91 = (f32[256,128]{1,0:T(8,128)S(1)}, f32[256,128]{1,0:T(8,128)S(1)}, f32[8,2,128]{2,1,0:T(2,128)S(1)}, f32[2,128]{1,0:T(2,128)S(1)}) custom-call(f32[256,128]{1,0:T(8,128)} %rewards_hbm.1, s32[256,128]{1,0:T(8,128)} %dones_hbm.1, f32[1,128]{1,0:T(1,128)} %bitcast.6, f32[1,128]{1,0:T(1,128)} %bitcast.7, f32[2,128]{1,0:T(2,128)} %iota.7.prior_hbm), custom_call_target="tpu_custom_call" | custom-call | tf_op jit(solution)/shard_map/pallas_call | solution.py:166
  14.7 1.4 %shard_map.92 = (f32[256,128]{1,0:T(8,128)}, f32[256,128]{1,0:T(8,128)}, f32[2]{0:T(128)}) custom-call(f32[256,128]{1,0:T(8,128)S(1)} %get-tuple-element.7.rewards, f32[256,128]{1,0:T(8,128)S(1)} %get-tuple-element.8.returns, f32[8,2,128]{2,1,0:T(2,128)S(1)} %get-tuple-element.9.ebuf, f32[2,128]{1,0:T(2,128)S(1)} %get-tuple-element.10.prior_ref), custom_call_target="tpu_custom_call" | custom-call | tf_op jit(solution)/shard_map/pallas_call | solution.py:187
  (1 shorter events, 0.0 us)

commit v4 on v2

--- a/solution.py
+++ b/solution.py
@@ -26,17 +26,16 @@
 
 def kernel(T, E, rewards_hbm, dones_hbm, horizon_hbm, bootstrap_hbm, mean_hbm, var_hbm,
            rewards, returns_ref, ebuf, prior_ref,
-           dones, horizon_ref, bootstrap_ref, mean_ref, var_ref, s_buf, p_buf, tbuf,
-           load_sem, tsend, trecv, esend, erecv):
+           dones, horizon_ref, bootstrap_ref, mean_ref, var_ref, s_buf, p_buf, tbuf, xbuf,
+           load_sem, tsend, trecv):
     t = lax.axis_index("tm")
     e = lax.axis_index("env")
     barrier = pltpu.get_barrier_semaphore()
-    for d in range(1, T):
-        pl.semaphore_signal(barrier, inc=1, device_id={"tm": lax.rem(t + d, T)},
-                            device_id_type=pl.DeviceIdType.MESH)
-    for d in range(1, E):
-        pl.semaphore_signal(barrier, inc=1, device_id={"env": lax.rem(e + d, E)},
-                            device_id_type=pl.DeviceIdType.MESH)
+    offsets = [(i, j) for i in range(T) for j in range(E) if i or j]
+    offsets.sort(key=lambda o: -min(o[0], T - o[0]))
+    peers = [{"tm": lax.rem(t + i, T), "env": lax.rem(e + j, E)} for i, j in offsets]
+    for peer in peers:
+        pl.semaphore_signal(barrier, inc=1, device_id=peer, device_id_type=pl.DeviceIdType.MESH)
     pairs = [(horizon_hbm, horizon_ref), (mean_hbm, mean_ref), (var_hbm, var_ref),
              (bootstrap_hbm, bootstrap_ref), (rewards_hbm, rewards),
              (dones_hbm, dones)]
@@ -74,61 +73,46 @@
     a = jnp.where(last, 0.0, pltpu.roll(full_s, SUB - 1, 0))
     b = jnp.where(last, 1.0, pltpu.roll(full_p, SUB - 1, 0))
     down = lambda value: jnp.sum(value, axis=0, keepdims=True)
-    tbuf[t, 0:1] = full_s[0:1]
-    tbuf[t, 1:2] = full_p[0:1]
-    tbuf[t, 2:3] = down(s1 + p1 * a)
-    tbuf[t, 3:4] = down(p1 * b)
-    tbuf[t, 4:5] = down(s2 + a * (2.0 * sp + a * p2))
-    tbuf[t, 5:6] = down(2.0 * b * (sp + a * p2))
-    tbuf[t, 6:7] = down(b * b * p2)
-    tbuf[t, 7:8] = jnp.zeros((1, lanes), jnp.float32)
-    pl.semaphore_wait(barrier, T + E - 2)
-    copies = []
-    for d in range(1, T):
-        copies.append(pltpu.make_async_remote_copy(
-            tbuf.at[t], tbuf.at[t], tsend.at[d - 1], trecv.at[d - 1],
-            device_id={"tm": lax.rem(t + d, T)}, device_id_type=pl.DeviceIdType.MESH))
+    tbuf[t, e, 0:1] = full_s[0:1]
+    tbuf[t, e, 1:2] = full_p[0:1]
+    tbuf[t, e, 2:3] = down(s1 + p1 * a)
+    tbuf[t, e, 3:4] = down(p1 * b)
+    tbuf[t, e, 4:5] = down(s2 + a * (2.0 * sp + a * p2))
+    tbuf[t, e, 5:6] = down(2.0 * b * (sp + a * p2))
+    tbuf[t, e, 6:7] = down(b * b * p2)
+    tbuf[t, e, 7:8] = bootstrap_ref[...]
+    pl.semaphore_wait(barrier, T * E - 1)
+    copies = [pltpu.make_async_remote_copy(
+        tbuf.at[t, e], tbuf.at[t, e], tsend.at[i], trecv.at[i],
+        device_id=peer, device_id_type=pl.DeviceIdType.MESH) for i, peer in enumerate(peers)]
     for copy in copies:
         copy.start()
     for copy in copies:
         copy.wait()
-    x = bootstrap_ref[...]
-    mine = x
-    first = jnp.zeros((1, lanes), jnp.float32)
-    second = jnp.zeros((1, lanes), jnp.float32)
+    x = tbuf[T - 1, :, 7]
+    first = jnp.zeros((E, lanes), jnp.float32)
+    second = jnp.zeros((E, lanes), jnp.float32)
     for j in reversed(range(T)):
-        mine = jnp.where(t == j, x, mine)
-        first = first + tbuf[j, 2:3] + tbuf[j, 3:4] * x
-        second = second + tbuf[j, 4:5] + x * (tbuf[j, 5:6] + x * tbuf[j, 6:7])
-        x = tbuf[j, 0:1] + tbuf[j, 1:2] * x
-    ebuf[e, 0:1] = first
-    ebuf[e, 1:2] = second
-    copies = []
-    for d in range(1, E):
-        copies.append(pltpu.make_async_remote_copy(
-            ebuf.at[e], ebuf.at[e], esend.at[d - 1], erecv.at[d - 1],
-            device_id={"env": lax.rem(e + d, E)}, device_id_type=pl.DeviceIdType.MESH))
-    for copy in copies:
-        copy.start()
+        xbuf[j] = x
+        first = first + tbuf[j, :, 2] + tbuf[j, :, 3] * x
+        second = second + tbuf[j, :, 4] + x * (tbuf[j, :, 5] + x * tbuf[j, :, 6])
+        x = tbuf[j, :, 0] + tbuf[j, :, 1] * x
+    mine = xbuf[t, pl.ds(e, 1), :]
+    ebuf[0] = first
+    ebuf[1] = second
     prior_ref[0:1] = center[0:1]
     prior_ref[1:2] = jnp.full((1, lanes), var_ref[0], jnp.float32)
     y = a + b * mine
     for k in range(chunk):
         returns_ref[pl.ds(k, SUB, stride=chunk), :] = s_buf[k] + p_buf[k] * y
-    for copy in copies:
-        copy.wait()
 
 
 def finish(T, E, rewards, returns, ebuf, prior_ref, out_rewards, out_returns, stats_ref,
            rewards_out, returns_out, sems):
     rows, lanes = rewards.shape
-    total = ebuf[0]
-    for j in range(1, E):
-        total = total + ebuf[j]
-    sums = jnp.sum(total, axis=1, keepdims=True)
+    first = jnp.sum(jnp.sum(ebuf[0], axis=0, keepdims=True), axis=1, keepdims=True)
+    second = jnp.sum(jnp.sum(ebuf[1], axis=0, keepdims=True), axis=1, keepdims=True)
     entries = jnp.float32(rows * T * lanes * E)
-    first = sums[0:1]
-    second = sums[1:2]
     mean0 = prior_ref[0:1, 0:1]
     var0 = prior_ref[1:2, 0:1]
     average = mean0 + first / entries
@@ -166,7 +150,7 @@
     kept, returns, sums, prior = pl.pallas_call(
         functools.partial(kernel, T, E),
         out_shape=(pltpu.VMEM(block, jnp.float32), pltpu.VMEM(block, jnp.float32),
-                   pltpu.VMEM((E, 2, lanes), jnp.float32), pltpu.VMEM((2, lanes), jnp.float32)),
+                   pltpu.VMEM((2, E, lanes), jnp.float32), pltpu.VMEM((2, lanes), jnp.float32)),
         in_specs=[hbm] * 6,
         out_specs=(vmem, vmem, vmem, vmem),
         scratch_shapes=[
@@ -177,12 +161,11 @@
             pltpu.SMEM((1,), jnp.float32),
             pltpu.VMEM((rows // SUB, SUB, lanes), jnp.float32),
             pltpu.VMEM((rows // SUB, SUB, lanes), jnp.float32),
-            pltpu.VMEM((T, ROWS, lanes), jnp.float32),
+            pltpu.VMEM((T, E, ROWS, lanes), jnp.float32),
+            pltpu.VMEM((T, E, lanes), jnp.float32),
             pltpu.SemaphoreType.DMA((6,)),
-            pltpu.SemaphoreType.DMA((T - 1,)),
-            pltpu.SemaphoreType.DMA((T - 1,)),
-            pltpu.SemaphoreType.DMA((E - 1,)),
-            pltpu.SemaphoreType.DMA((E - 1,)),
+            pltpu.SemaphoreType.DMA((T * E - 1,)),
+            pltpu.SemaphoreType.DMA((T * E - 1,)),
         ],
         compiler_params=pltpu.CompilerParams(collective_id=0, has_side_effects=True),
     )(rewards, dones, horizon.reshape(1, lanes), bootstrap.reshape(1, lanes), prior_mean, prior_var)

time: 15.7 us -> 15.1 us (0.962)
  Pallas kernels: 13.6 us -> 13 us
    pallas_call x1, Pallas kernels: 12.2 us -> 11.6 us  [local(): pl.pallas_call(functools.partial(kernel, T, E), out_shape=(pltpu.VMEM(blo...]
where the time goes in v4:
time: 15.1 us; the launch traced here: 14.9 us
  Pallas kernels  13 us (86%)
  between operations  1.93 us (13%)
    pallas_call x1, Pallas kernels, local(): pl.pallas_call(functools.partial(kernel, T, E), out_shape=(pltpu.VMEM(blo...  11.6 us
    pallas_call x1, Pallas kernels, local(): pl.pallas_call(functools.partial(finish, T, E), out_shape=(jax.ShapeDtype...  1.42 us

profile of v4, /device:TPU:0, one launch (start us, length us, event | category | flops | bytes accessed | tf_op | source)
XLA Modules:
  0.0 14.9 jit_solution(2497646547430215869)
XLA Ops:
  1.9 11.6 %shard_map.85 = (f32[256,128]{1,0:T(8,128)S(1)}, f32[256,128]{1,0:T(8,128)S(1)}, f32[2,8,128]{2,1,0:T(8,128)S(1)}, f32[2,128]{1,0:T(2,128)S(1)}) custom-call(f32[256,128]{1,0:T(8,128)} %rewards_hbm.1, s32[256,128]{1,0:T(8,128)} %dones_hbm.1, f32[1,128]{1,0:T(1,128)} %bitcast.2, f32[1,128]{1,0:T(1,128)} %bitcast.3, f32[1]{0:T(128)S(6)} %copy.9.mean_hbm, ...), custom_call_target="tpu_custom_call" | custom-call | tf_op jit(solution)/shard_map/pallas_call | solution.py:150
  13.5 1.4 %shard_map.86 = (f32[256,128]{1,0:T(8,128)}, f32[256,128]{1,0:T(8,128)}, f32[2]{0:T(128)}) custom-call(f32[256,128]{1,0:T(8,128)S(1)} %get-tuple-element.7.rewards, f32[256,128]{1,0:T(8,128)S(1)} %get-tuple-element.8.returns, f32[2,8,128]{2,1,0:T(8,128)S(1)} %get-tuple-element.9.ebuf, f32[2,128]{1,0:T(2,128)S(1)} %get-tuple-element.10.prior_ref), custom_call_target="tpu_custom_call" | custom-call | tf_op jit(solution)/shard_map/pallas_call | solution.py:172

commit v5 on v4

--- a/solution.py
+++ b/solution.py
@@ -9,7 +9,7 @@
 
 SUB = 8
 ROWS = 8
-PARTS = 4
+PARTS = 2
 
 
 def compose_rows(summed, product, row):
@@ -25,8 +25,8 @@
 
 
 def kernel(T, E, rewards_hbm, dones_hbm, horizon_hbm, bootstrap_hbm, mean_hbm, var_hbm,
-           rewards, returns_ref, ebuf, prior_ref,
-           dones, horizon_ref, bootstrap_ref, mean_ref, var_ref, s_buf, p_buf, tbuf, xbuf,
+           rewards, s_buf, p_buf, carry_ref, ebuf, prior_ref,
+           dones, horizon_ref, bootstrap_ref, mean_ref, var_ref, tbuf, xbuf,
            load_sem, tsend, trecv):
     t = lax.axis_index("tm")
     e = lax.axis_index("env")
@@ -102,41 +102,46 @@
     ebuf[1] = second
     prior_ref[0:1] = center[0:1]
     prior_ref[1:2] = jnp.full((1, lanes), var_ref[0], jnp.float32)
-    y = a + b * mine
-    for k in range(chunk):
-        returns_ref[pl.ds(k, SUB, stride=chunk), :] = s_buf[k] + p_buf[k] * y
-
-
-def finish(T, E, rewards, returns, ebuf, prior_ref, out_rewards, out_returns, stats_ref,
-           rewards_out, returns_out, sems):
+    carry_ref[...] = a + b * mine
+
+
+def finish(T, E, rewards, s_buf, p_buf, carry_ref, ebuf, prior_ref, out_rewards, out_returns, out_stats,
+           rewards_out, returns_out, stats, sems):
     rows, lanes = rewards.shape
+    chunk = rows // SUB
     first = jnp.sum(jnp.sum(ebuf[0], axis=0, keepdims=True), axis=1, keepdims=True)
     second = jnp.sum(jnp.sum(ebuf[1], axis=0, keepdims=True), axis=1, keepdims=True)
-    entries = jnp.float32(rows * T * lanes * E)
+    entries = float(rows * T * lanes * E)
+    prior_count = entries
+    merged = prior_count + entries
     mean0 = prior_ref[0:1, 0:1]
     var0 = prior_ref[1:2, 0:1]
-    average = mean0 + first / entries
-    spread = second - first * first / entries
-    prior_count = entries
-    merged = prior_count + entries
-    delta = average - mean0
-    new_mean = mean0 + delta * entries / merged
-    new_spread = var0 * prior_count + spread + delta * delta * prior_count * entries / merged
-    variance = new_spread / merged
-    inverse = jnp.broadcast_to(1.0 / jnp.sqrt(variance + 1e-08), (SUB, lanes))
+    delta = first * (1.0 / entries)
+    spread = second - first * delta
+    new_mean = mean0 + delta * (entries / merged)
+    variance = (var0 * (prior_count / merged) + spread * (1.0 / merged)
+                + delta * delta * (prior_count / merged * (entries / merged)))
+    inverse = jnp.broadcast_to(lax.rsqrt(variance + 1e-08), (SUB, lanes))
     copies = []
+
+    def send(source, target, rank):
+        copy = pltpu.make_async_copy(source, target, sems.at[rank])
+        copy.start()
+        copies.append(copy)
+
+    y = carry_ref[...] * inverse
+    for k in range(chunk):
+        returns_out[pl.ds(k, SUB, stride=chunk), :] = s_buf[k] * inverse + p_buf[k] * y
+    send(returns_out, out_returns, 0)
     part = rows // PARTS
     for i in range(PARTS):
-        for n, (source, staged, target) in enumerate(
-                ((rewards, rewards_out, out_rewards), (returns, returns_out, out_returns))):
-            for k in range(i * part, (i + 1) * part, SUB):
-                staged[k:k + SUB] = source[k:k + SUB] * inverse
-            where = pl.ds(i * part, part)
-            copy = pltpu.make_async_copy(staged.at[where], target.at[where], sems.at[n, i])
-            copy.start()
-            copies.append(copy)
-    stats_ref[0] = new_mean[0, 0]
-    stats_ref[1] = variance[0, 0]
+        for k in range(i * part, (i + 1) * part, SUB):
+            rewards_out[k:k + SUB] = rewards[k:k + SUB] * inverse
+        where = pl.ds(i * part, part)
+        send(rewards_out.at[where], out_rewards.at[where], 2 + i)
+    stats[0] = new_mean[0, 0]
+    stats[1] = variance[0, 0]
+    send(stats, out_stats, 1)
     for copy in copies:
         copy.wait()
 
@@ -145,22 +150,22 @@
     rows, lanes = rewards.shape
     block = (rows, lanes)
     vmem = pl.BlockSpec(memory_space=pltpu.VMEM)
-    smem = pl.BlockSpec(memory_space=pltpu.SMEM)
     hbm = pl.BlockSpec(memory_space=pltpu.HBM)
-    kept, returns, sums, prior = pl.pallas_call(
+    kept, summed, product, carry, sums, prior = pl.pallas_call(
         functools.partial(kernel, T, E),
-        out_shape=(pltpu.VMEM(block, jnp.float32), pltpu.VMEM(block, jnp.float32),
+        out_shape=(pltpu.VMEM(block, jnp.float32),
+                   pltpu.VMEM((rows // SUB, SUB, lanes), jnp.float32),
+                   pltpu.VMEM((rows // SUB, SUB, lanes), jnp.float32),
+                   pltpu.VMEM((SUB, lanes), jnp.float32),
                    pltpu.VMEM((2, E, lanes), jnp.float32), pltpu.VMEM((2, lanes), jnp.float32)),
         in_specs=[hbm] * 6,
-        out_specs=(vmem, vmem, vmem, vmem),
+        out_specs=(vmem,) * 6,
         scratch_shapes=[
             pltpu.VMEM(block, jnp.int32),
             pltpu.VMEM((1, lanes), jnp.float32),
             pltpu.VMEM((1, lanes), jnp.float32),
             pltpu.SMEM((1,), jnp.float32),
             pltpu.SMEM((1,), jnp.float32),
-            pltpu.VMEM((rows // SUB, SUB, lanes), jnp.float32),
-            pltpu.VMEM((rows // SUB, SUB, lanes), jnp.float32),
             pltpu.VMEM((T, E, ROWS, lanes), jnp.float32),
             pltpu.VMEM((T, E, lanes), jnp.float32),
             pltpu.SemaphoreType.DMA((6,)),
@@ -174,15 +179,16 @@
         out_shape=(jax.ShapeDtypeStruct(block, jnp.float32),
                    jax.ShapeDtypeStruct(block, jnp.float32),
                    jax.ShapeDtypeStruct((2,), jnp.float32)),
-        in_specs=[vmem] * 4,
-        out_specs=(hbm, hbm, smem),
+        in_specs=[vmem] * 6,
+        out_specs=(hbm, hbm, hbm),
         scratch_shapes=[
             pltpu.VMEM(block, jnp.float32),
             pltpu.VMEM(block, jnp.float32),
-            pltpu.SemaphoreType.DMA((2, PARTS)),
+            pltpu.SMEM((2,), jnp.float32),
+            pltpu.SemaphoreType.DMA((2 + PARTS,)),
         ],
         compiler_params=pltpu.CompilerParams(vmem_limit_bytes=4 * 2**20),
-    )(kept, returns, sums, prior)
+    )(kept, summed, product, carry, sums, prior)
 
 
 def solution(mesh):

time: 15.1 us -> 14.6 us (0.967)
  Pallas kernels: 13 us -> 12.5 us
    pallas_call x1, Pallas kernels: 1.42 us -> 0.95 us  [local(): pl.pallas_call(functools.partial(finish, T, E), out_shape=(jax.ShapeDtype...]
where the time goes in v5:
time: 14.6 us; the launch traced here: 14.4 us
  Pallas kernels  12.5 us (86%)
  between operations  1.93 us (13%)
    pallas_call x1, Pallas kernels, local(): pl.pallas_call(functools.partial(kernel, T, E), out_shape=(pltpu.VMEM(blo...  11.5 us
    pallas_call x1, Pallas kernels, local(): pl.pallas_call(functools.partial(finish, T, E), out_shape=(jax.ShapeDtype...  0.95 us

profile of v5, /device:TPU:0, one launch (start us, length us, event | category | flops | bytes accessed | tf_op | source)
XLA Modules:
  0.0 14.4 jit_solution(198857032433057544)
XLA Ops:
  1.9 11.5 %shard_map.85 = (f32[256,128]{1,0:T(8,128)S(1)}, f32[32,8,128]{2,1,0:T(8,128)S(1)}, f32[32,8,128]{2,1,0:T(8,128)S(1)}, f32[8,128]{1,0:T(8,128)S(1)}, f32[2,8,128]{2,1,0:T(8,128)S(1)}, /*index=5*/f32[2,128]{1,0:T(2,128)S(1)}) custom-call(f32[256,128]{1,0:T(8,128)} %rewards_hbm.1, s32[256,128]{1,0:T(8,128)} %dones_hbm.1, f32[1,128]{1,0:T(1,128)} %bitcast.2, ...), custom_call_target="tpu_custom_call" | custom-call | tf_op jit(solution)/shard_map/pallas_call | solution.py:154
  13.4 1.0 %shard_map.86 = (f32[256,128]{1,0:T(8,128)}, f32[256,128]{1,0:T(8,128)}, f32[2]{0:T(128)}) custom-call(f32[256,128]{1,0:T(8,128)S(1)} %get-tuple-element.9.rewards, f32[32,8,128]{2,1,0:T(8,128)S(1)} %get-tuple-element.10.s_buf, f32[32,8,128]{2,1,0:T(8,128)S(1)} %get-tuple-element.11.p_buf, f32[8,128]{1,0:T(8,128)S(1)} %get-tuple-element.12.carry_ref, ...), custom_call_target="tpu_custom_call" | custom-call | tf_op jit(solution)/shard_map/pallas_call | solution.py:177

commit v6 on v5

--- a/solution.py
+++ b/solution.py
@@ -9,6 +9,7 @@
 
 SUB = 8
 ROWS = 8
+SENT = 7
 PARTS = 2
 
 
@@ -73,23 +74,25 @@
     a = jnp.where(last, 0.0, pltpu.roll(full_s, SUB - 1, 0))
     b = jnp.where(last, 1.0, pltpu.roll(full_p, SUB - 1, 0))
     down = lambda value: jnp.sum(value, axis=0, keepdims=True)
-    tbuf[t, e, 0:1] = full_s[0:1]
+    known = jnp.where(t == T - 1, bootstrap_ref[...], jnp.zeros((1, lanes), jnp.float32))
+    a = a + b * known
+    rest = sp + a * p2
+    tbuf[t, e, 0:1] = full_s[0:1] + full_p[0:1] * known
     tbuf[t, e, 1:2] = full_p[0:1]
     tbuf[t, e, 2:3] = down(s1 + p1 * a)
     tbuf[t, e, 3:4] = down(p1 * b)
-    tbuf[t, e, 4:5] = down(s2 + a * (2.0 * sp + a * p2))
-    tbuf[t, e, 5:6] = down(2.0 * b * (sp + a * p2))
+    tbuf[t, e, 4:5] = down(s2 + a * (sp + rest))
+    tbuf[t, e, 5:6] = down(2.0 * b * rest)
     tbuf[t, e, 6:7] = down(b * b * p2)
-    tbuf[t, e, 7:8] = bootstrap_ref[...]
     pl.semaphore_wait(barrier, T * E - 1)
     copies = [pltpu.make_async_remote_copy(
-        tbuf.at[t, e], tbuf.at[t, e], tsend.at[i], trecv.at[i],
+        tbuf.at[t, e, 0:SENT], tbuf.at[t, e, 0:SENT], tsend.at[i], trecv.at[i],
         device_id=peer, device_id_type=pl.DeviceIdType.MESH) for i, peer in enumerate(peers)]
     for copy in copies:
         copy.start()
     for copy in copies:
         copy.wait()
-    x = tbuf[T - 1, :, 7]
+    x = jnp.zeros((E, lanes), jnp.float32)
     first = jnp.zeros((E, lanes), jnp.float32)
     second = jnp.zeros((E, lanes), jnp.float32)
     for j in reversed(range(T)):

time: 14.6 us -> 14.4 us (0.986)
  Pallas kernels: 12.5 us -> 12.3 us
    pallas_call x1, Pallas kernels: 11.5 us -> 11.3 us  [local(): pl.pallas_call(functools.partial(kernel, T, E), out_shape=(pltpu.VMEM(blo...]
where the time goes in v6:
time: 14.4 us; the launch traced here: 14.2 us
  Pallas kernels  12.3 us (85%)
  between operations  1.93 us (13%)
    pallas_call x1, Pallas kernels, local(): pl.pallas_call(functools.partial(kernel, T, E), out_shape=(pltpu.VMEM(blo...  11.3 us
    pallas_call x1, Pallas kernels, local(): pl.pallas_call(functools.partial(finish, T, E), out_shape=(jax.ShapeDtype...  0.95 us

profile of v6, /device:TPU:0, one launch (start us, length us, event | category | flops | bytes accessed | tf_op | source)
XLA Modules:
  0.0 14.2 jit_solution(4856736181771444968)
XLA Ops:
  1.9 11.3 %shard_map.85 = (f32[256,128]{1,0:T(8,128)S(1)}, f32[32,8,128]{2,1,0:T(8,128)S(1)}, f32[32,8,128]{2,1,0:T(8,128)S(1)}, f32[8,128]{1,0:T(8,128)S(1)}, f32[2,8,128]{2,1,0:T(8,128)S(1)}, /*index=5*/f32[2,128]{1,0:T(2,128)S(1)}) custom-call(f32[256,128]{1,0:T(8,128)} %rewards_hbm.1, s32[256,128]{1,0:T(8,128)} %dones_hbm.1, f32[1,128]{1,0:T(1,128)} %bitcast.2, ...), custom_call_target="tpu_custom_call" | custom-call | tf_op jit(solution)/shard_map/pallas_call | solution.py:157
  13.2 1.0 %shard_map.86 = (f32[256,128]{1,0:T(8,128)}, f32[256,128]{1,0:T(8,128)}, f32[2]{0:T(128)}) custom-call(f32[256,128]{1,0:T(8,128)S(1)} %get-tuple-element.9.rewards, f32[32,8,128]{2,1,0:T(8,128)S(1)} %get-tuple-element.10.s_buf, f32[32,8,128]{2,1,0:T(8,128)S(1)} %get-tuple-element.11.p_buf, f32[8,128]{1,0:T(8,128)S(1)} %get-tuple-element.12.carry_ref, ...), custom_call_target="tpu_custom_call" | custom-call | tf_op jit(solution)/shard_map/pallas_call | solution.py:180
